TPU v7x, 32 devices: a whole 2x2x4 slice. The times are simulated.
32 devices in a mesh: rep: 2 (over x), fsdp: 16 (over z, y, core).
Axes of the slice: x: 2, y: 2, z: 4, core: 2. Of those that a mesh axis runs over, the one named last changes fastest.
Arguments:
- tokens: bfloat16 [256, 3584], P(('rep', 'fsdp')), may hold values from -6 to 6
- targets: bfloat16 [256, 3584], P(('rep', 'fsdp')), may hold values from -6 to 6
- gate_weight: bfloat16 [3584, 18944], P(None, 'fsdp'), may hold values from -0.09375 to 0.09375
- up_weight: bfloat16 [3584, 18944], P(None, 'fsdp'), may hold values from -0.09375 to 0.09375
- down_weight: bfloat16 [18944, 3584], P('fsdp'), may hold values from -0.046875 to 0.046875
- gate_direction: bfloat16 [3584, 18944], P(None, 'fsdp'), may hold values from -0.09375 to 0.09375
- up_direction: bfloat16 [3584, 18944], P(None, 'fsdp'), may hold values from -0.09375 to 0.09375
- down_direction: bfloat16 [18944, 3584], P('fsdp'), may hold values from -0.046875 to 0.046875
Outputs:
- hvp_gate: float32 [3584, 18944], P(None, 'fsdp')
- hvp_up: float32 [3584, 18944], P(None, 'fsdp')
- hvp_down: float32 [18944, 3584], P('fsdp')
All inputs are finite; a program needn't handle non-finite values.
Results may differ from a plain program's by a relative error of at most 0.0069.
Values may be sent and summed in bfloat16 or wider, within the bound.
A program may use at most 192 MiB of HBM per device.

v0:
```python
import jax
import jax.numpy as jnp
from jax import lax
from jax.sharding import PartitionSpec as P


def silu_parts(gate):
    sigmoid_value = jax.nn.sigmoid(gate)
    slope = sigmoid_value * (1.0 + gate * (1.0 - sigmoid_value))
    bend = sigmoid_value * (1.0 - sigmoid_value) * (2.0 + gate * (1.0 - 2.0 * sigmoid_value))
    return (gate * sigmoid_value, slope, bend)


def inner_rows(left, right):
    return lax.dot_general(
        left, right, (((0,), (0,)), ((), ())), preferred_element_type=jnp.float32
    )


def products(
    gathered,
    gate_grad_tangent,
    up_grad_tangent,
    hidden,
    hidden_tangent,
    error_all,
    error_tangent_all,
):
    hvp_gate = inner_rows(gathered, gate_grad_tangent)
    hvp_up = inner_rows(gathered, up_grad_tangent)
    hvp_down = inner_rows(hidden_tangent, error_all) + inner_rows(hidden, error_tangent_all)
    return (hvp_gate, hvp_up, hvp_down)


def on_device(
    tokens,
    targets,
    gate_weight,
    up_weight,
    down_weight,
    gate_direction,
    up_direction,
    down_direction,
):
    width = tokens.shape[1]
    gathered = lax.all_gather(tokens, "fsdp", axis=0, tiled=True)
    gate = jnp.dot(gathered, gate_weight, preferred_element_type=jnp.float32)
    up = jnp.dot(gathered, up_weight, preferred_element_type=jnp.float32)
    gate_tangent = jnp.dot(gathered, gate_direction, preferred_element_type=jnp.float32)
    up_tangent = jnp.dot(gathered, up_direction, preferred_element_type=jnp.float32)
    activation, slope, bend = silu_parts(gate)
    hidden = (activation * up).astype(jnp.bfloat16)
    hidden_tangent = (slope * gate_tangent * up + activation * up_tangent).astype(jnp.bfloat16)
    primal = jnp.dot(hidden, down_weight, preferred_element_type=jnp.float32)
    tangent = jnp.dot(hidden_tangent, down_weight, preferred_element_type=jnp.float32) + jnp.dot(
        hidden, down_direction, preferred_element_type=jnp.float32
    )
    summed = lax.psum_scatter(
        jnp.concatenate([primal, tangent], axis=1), "fsdp", scatter_dimension=0, tiled=True
    )
    error = (summed[:, :width] - targets.astype(jnp.float32)).astype(jnp.bfloat16)
    error_tangent = summed[:, width:].astype(jnp.bfloat16)
    error_all, error_tangent_all = (
        lax.all_gather(error, "fsdp", axis=0, tiled=True),
        lax.all_gather(error_tangent, "fsdp", axis=0, tiled=True),
    )
    back = jnp.dot(error_all, down_weight.T, preferred_element_type=jnp.float32)
    back_tangent = jnp.dot(
        error_tangent_all, down_weight.T, preferred_element_type=jnp.float32
    ) + jnp.dot(error_all, down_direction.T, preferred_element_type=jnp.float32)
    gate_grad_tangent = (
        back_tangent * up * slope + back * up_tangent * slope + back * up * bend * gate_tangent
    ).astype(jnp.bfloat16)
    up_grad_tangent = (back_tangent * activation + back * slope * gate_tangent).astype(jnp.bfloat16)
    pair_rows = (
        lax.all_gather(gathered, "rep", axis=0, tiled=True),
        lax.all_gather(gate_grad_tangent, "rep", axis=0, tiled=True),
        lax.all_gather(up_grad_tangent, "rep", axis=0, tiled=True),
        lax.all_gather(hidden, "rep", axis=0, tiled=True),
        lax.all_gather(hidden_tangent, "rep", axis=0, tiled=True),
        lax.all_gather(error_all, "rep", axis=0, tiled=True),
        lax.all_gather(error_tangent_all, "rep", axis=0, tiled=True),
    )
    hvp_gate, hvp_up, hvp_down = products(
        pair_rows[0],
        pair_rows[1],
        pair_rows[2],
        pair_rows[3],
        pair_rows[4],
        pair_rows[5],
        pair_rows[6],
    )
    return (hvp_gate, hvp_up, hvp_down)


def solution(mesh):
    in_specs = (
        P(("rep", "fsdp"), None),
        P(("rep", "fsdp"), None),
        P(None, "fsdp"),
        P(None, "fsdp"),
        P("fsdp", None),
        P(None, "fsdp"),
        P(None, "fsdp"),
        P("fsdp", None),
    )
    out_specs = (P(None, "fsdp"), P(None, "fsdp"), P("fsdp", None))
    return jax.shard_map(
        on_device, mesh=mesh, in_specs=in_specs, out_specs=out_specs, check_vma=False
    )
```

profile of v0, /device:TPU:0, one launch (start us, length us, event | category | flops | bytes accessed | tf_op | source)
XLA Modules:
  0.0 296.1 jit_solution(9094616543245920694)
XLA Ops:
  8.0 26.1 %all_gather.30 = bf16[128,3584]{1,0:T(8,128)(2,1)S(1)} all-gather(bf16[8,3584]{1,0:T(8,128)(2,1)} %param.8), channel_id=1, replica_groups=mesh['rep'=2,'fsdp'=16] {'fsdp'}, dimensions={0}, use_global_device_ids=true | all-gather | bytes 974848 | tf_op jit(solution)/shard_map/all_gather | solution.py:46
  34.2 6.1 %fusion.12 = f32[128,1184]{0,1:T(8,128)S(1)} fusion(bf16[128,3584]{1,0:T(8,128)(2,1)S(1)} %all_gather.30, bf16[3584,1184]{0,1:T(8,128)(2,1)} %param.14), kind=kOutput, calls=%fused_computation.26 | convolution fusion | flops 1086324736 | bytes 10010624 | tf_op jit(solution)/shard_map/dot_general | solution.py:50
  40.4 2.4 fusion.11
  42.8 0.2 slice-done.7
  43.0 0.1 slice-done.8
  43.0 2.4 fusion.9
  45.4 0.4 slice-done.10
  45.8 3.3 %multiply_convert_fusion = (bf16[128,1184]{0,1:T(8,128)(2,1)S(1)}, bf16[128,1184]{0,1:T(8,128)(2,1)S(1)}, f32[128,1184]{0,1:T(8,128)}) fusion(f32[128,1184]{0,1:T(8,128)S(1)} %fusion.9, f32[128,1184]{0,1:T(8,128)S(1)} %fusion.12, f32[128,1184]{0,1:T(8,128)S(1)} %fusion.11, bf16[128,3584]{1,0:T(8,128)(2,1)S(1)} %all_gather.30, ...), kind=kOutput, calls=%fused_computation.17 | convolution fusion | flops 1088598016 | bytes 12435456 | tf_op jit(solution)/shard_map/dot_general | solution.py:48
  49.1 1.4 fusion.13
  50.5 1.4 fusion.10
  51.9 0.7 slice-done.4
  52.6 0.1 slice-done.5
  52.6 1.4 convolution_add_fusion.1
  54.0 2.1 pad_maximum_fusion
  56.2 0.5 all-gather.4.cloned.1.call-update
  56.8 65.3 %reduce-scatter.2.cloned.1.call-done = f32[8,7168]{1,0:T(8,128)} async-done(((f32[128,7168]{1,0:T(8,128)}), f32[8,7168]{1,0:T(8,128)}) %reduce-scatter.2.cloned.1.call-update) | async-done | bytes 229392 | tf_op jit(solution)/shard_map/reduce_scatter | solution.py:58
  122.1 0.9 fusion.8
  123.0 23.4 %all_gather.32 = bf16[128,3584]{1,0:T(8,128)(2,1)} all-gather(bf16[8,3584]{1,0:T(8,128)(2,1)S(1)} %fusion.8), channel_id=1, replica_groups=mesh['rep'=2,'fsdp'=16] {'fsdp'}, dimensions={0}, use_global_device_ids=true | all-gather | bytes 974848 | tf_op jit(solution)/shard_map/all_gather | solution.py:64
  146.4 0.0 all-gather.8.cloned.1.call-start
  146.4 13.5 %all_gather.36 = bf16[256,1184]{0,1:T(8,128)(2,1)S(1)} all-gather(bf16[128,1184]{0,1:T(8,128)(2,1)S(1)} %get-tuple-element.6), channel_id=1, replica_groups=mesh['rep'=2,'fsdp'=16] {'rep'}, dimensions={0}, use_global_device_ids=true | all-gather | bytes 909312 | tf_op jit(solution)/shard_map/all_gather | solution.py:80
  159.9 17.0 %all_gather.38 = bf16[256,1184]{0,1:T(8,128)(2,1)S(1)} all-gather(bf16[128,1184]{0,1:T(8,128)(2,1)S(1)} %get-tuple-element.5), channel_id=1, replica_groups=mesh['rep'=2,'fsdp'=16] {'rep'}, dimensions={0}, use_global_device_ids=true | all-gather | bytes 909312 | tf_op jit(solution)/shard_map/all_gather | solution.py:79
  176.9 0.9 slice.15
  177.8 20.2 %all_gather.31 = bf16[128,3584]{1,0:T(8,128)(2,1)S(1)} all-gather(bf16[8,3584]{1,0:T(8,128)(2,1)S(1)} %slice.15), channel_id=1, replica_groups=mesh['rep'=2,'fsdp'=16] {'fsdp'}, dimensions={0}, use_global_device_ids=true | all-gather | bytes 974848 | tf_op jit(solution)/shard_map/all_gather | solution.py:65
  198.1 7.0 %fusion.14 = f32[128,1184]{0,1:T(8,128)} fusion(bf16[128,3584]{1,0:T(8,128)(2,1)S(1)} %all_gather.31, bf16[1184,3584]{1,0:T(8,128)(2,1)} %param.12), kind=kOutput, calls=%fused_computation.28 | convolution fusion | flops 1086324736 | bytes 10010624 | tf_op jit(solution)/shard_map/dot_general | solution.py:68
  205.1 6.0 %convolution_add_fusion.2 = f32[128,1184]{0,1:T(8,128)S(1)} fusion(f32[128,1184]{0,1:T(8,128)} %fusion.14, bf16[128,3584]{1,0:T(8,128)(2,1)S(1)} %copy-done.3, bf16[1184,3584]{1,0:T(8,128)(2,1)} %param.15), kind=kOutput, calls=%fused_computation.5 | convolution fusion | flops 1086476288 | bytes 10616832 | tf_op jit(solution)/shard_map/dot_general | solution.py:70
  211.2 6.4 %add_convert_fusion = (bf16[128,1184]{0,1:T(8,128)(2,1)S(1)}, bf16[128,1184]{0,1:T(8,128)(2,1)S(1)}) fusion(f32[128,1184]{0,1:T(8,128)S(1)} %copy-done.8, f32[128,1184]{0,1:T(8,128)S(1)} %convolution_add_fusion.2, f32[128,1184]{0,1:T(8,128)S(1)} %copy-done.10, f32[128,1184]{0,1:T(8,128)S(1)} %copy-done.11, f32[128,1184]{0,1:T(8,128)S(1)} %copy-done.6, ...), kind=kOutput, calls=%fused_computation.15 | convolution fusion | flops 1090568192 | bytes 13041664 | tf_op jit(solution)/shard_map/dot_general | solution.py:67
  217.6 17.2 %all_gather.33 = bf16[256,1184]{0,1:T(8,128)(2,1)S(1)} all-gather(bf16[128,1184]{0,1:T(8,128)(2,1)S(1)} %get-tuple-element.4), channel_id=1, replica_groups=mesh['rep'=2,'fsdp'=16] {'rep'}, dimensions={0}, use_global_device_ids=true | all-gather | bytes 909312 | tf_op jit(solution)/shard_map/all_gather | solution.py:77
  234.7 10.2 %convolution_bitcast_fusion.1 = f32[3584,1184]{0,1:T(8,128)} fusion(bf16[256,1184]{0,1:T(8,128)(2,1)S(1)} %all_gather.33, bf16[256,3584]{1,0:T(8,128)(2,1)} %all-gather.4.cloned.1.call-done), kind=kOutput, calls=%fused_computation.2 | convolution fusion | flops 2172649472 | bytes 19415040 | tf_op jit(solution)/shard_map/dot_general | solution.py:15
  245.0 9.9 %all_gather.35 = bf16[256,1184]{0,1:T(8,128)(2,1)S(1)} all-gather(bf16[128,1184]{0,1:T(8,128)(2,1)S(1)} %get-tuple-element.3), channel_id=1, replica_groups=mesh['rep'=2,'fsdp'=16] {'rep'}, dimensions={0}, use_global_device_ids=true | all-gather | bytes 909312 | tf_op jit(solution)/shard_map/all_gather | solution.py:78
  254.9 8.6 %convolution_bitcast_fusion = f32[3584,1184]{0,1:T(8,128)} fusion(bf16[256,1184]{0,1:T(8,128)(2,1)S(1)} %all_gather.35, bf16[256,3584]{1,0:T(8,128)(2,1)S(1)} %copy-done.4), kind=kOutput, calls=%fused_computation.1 | convolution fusion | flops 2172649472 | bytes 19415040 | tf_op jit(solution)/shard_map/dot_general | solution.py:15
  263.5 10.1 %fusion.15 = f32[1184,3584]{1,0:T(8,128)} fusion(bf16[256,1184]{0,1:T(8,128)(2,1)S(1)} %all_gather.36, bf16[256,3584]{1,0:T(8,128)(2,1)} %all-gather.6.cloned.1.call-done), kind=kOutput, calls=%fused_computation.29 | convolution fusion | flops 2172649472 | bytes 19415040 | tf_op jit(solution)/shard_map/dot_general | solution.py:15
  273.6 15.0 %convolution_add_fusion = f32[1184,3584]{1,0:T(8,128)} fusion(f32[1184,3584]{1,0:T(8,128)} %fusion.15, bf16[256,1184]{0,1:T(8,128)(2,1)S(1)} %all_gather.38, bf16[256,3584]{1,0:T(8,128)(2,1)} %all-gather.8.cloned.1.call-done), kind=kOutput, calls=%fused_computation | convolution fusion | flops 2176892928 | bytes 36388864 | tf_op jit(solution)/shard_map/dot_general | solution.py:15
  (58 shorter events, 0.3 us)
Async XLA Ops:
  8.0 114.1 %reduce-scatter.2.cloned.1.call-start = ((), (), s32[]{:S(2)}) async-start(), calls=%async_computation.1 | async-start | bytes 3899392 | tf_op jit(solution)/shard_map/reduce_scatter | solution.py:58
  34.2 11.2 %copy-start = (bf16[128,3584]{1,0:T(8,128)(2,1)}, bf16[128,3584]{1,0:T(8,128)(2,1)S(1)}, u32[]{:S(2)}) copy-start(bf16[128,3584]{1,0:T(8,128)(2,1)S(1)} %all_gather.30) | copy-start | bytes 2752516
  34.2 6.2 %copy-start.1 = (bf16[3584,1184]{0,1:T(8,128)(2,1)S(1)}, bf16[3584,1184]{0,1:T(8,128)(2,1)}, u32[]{:S(2)}) copy-start(bf16[3584,1184]{0,1:T(8,128)(2,1)} %param.13) | copy-start | bytes 25460740
  34.2 8.6 %slice-start.6 = ((s8[8486912]{0:T(1024)(128)(4,1)}), s8[4194304]{0:T(1024)(128)(4,1)S(1)}, s32[]{:S(2)}) async-start(s8[8486912]{0:T(1024)(128)(4,1)} %bitcast.36), calls=%async_computation.11 | async-start | bytes 8388608
  34.2 8.8 %slice-start.7 = ((s8[8486912]{0:T(1024)(128)(4,1)}), s8[4194304]{0:T(1024)(128)(4,1)S(1)}, s32[]{:S(2)}) async-start(s8[8486912]{0:T(1024)(128)(4,1)} %bitcast.36), calls=%async_computation.12 | async-start | bytes 8388608
  40.4 5.0 %copy-start.5 = (f32[128,1184]{0,1:T(8,128)}, f32[128,1184]{0,1:T(8,128)S(1)}, u32[]{:S(2)}) copy-start(f32[128,1184]{0,1:T(8,128)S(1)} %fusion.12) | copy-start | bytes 1818628
  40.4 2.6 slice-start.8
  40.4 5.0 %slice-start.9 = ((s8[8486912]{0:T(1024)(128)(4,1)}), s8[4194304]{0:T(1024)(128)(4,1)S(1)}, s32[]{:S(2)}) async-start(s8[8486912]{0:T(1024)(128)(4,1)} %bitcast.38), calls=%async_computation.14 | async-start | bytes 8388608
  40.4 5.4 %slice-start.10 = ((s8[8486912]{0:T(1024)(128)(4,1)}), s8[4194304]{0:T(1024)(128)(4,1)S(1)}, s32[]{:S(2)}) async-start(s8[8486912]{0:T(1024)(128)(4,1)} %bitcast.38), calls=%async_computation.15 | async-start | bytes 8388608
  43.0 2.4 copy-start.7
  43.0 2.8 slice-start.11
  43.0 6.0 %slice-start = ((s8[8486912]{0:T(1024)(128)(4,1)}), s8[4194304]{0:T(1024)(128)(4,1)S(1)}, s32[]{:S(2)}) async-start(s8[8486912]{0:T(1024)(128)(4,1)} %bitcast.32), calls=%async_computation.5 | async-start | bytes 8388608
  43.0 6.0 %slice-start.1 = ((s8[8486912]{0:T(1024)(128)(4,1)}), s8[4194304]{0:T(1024)(128)(4,1)S(1)}, s32[]{:S(2)}) async-start(s8[8486912]{0:T(1024)(128)(4,1)} %bitcast.32), calls=%async_computation.6 | async-start | bytes 8388608
  45.8 3.3 %copy-start.9 = (f32[128,1184]{0,1:T(8,128)}, f32[128,1184]{0,1:T(8,128)S(1)}, u32[]{:S(2)}) copy-start(f32[128,1184]{0,1:T(8,128)S(1)} %fusion.9) | copy-start | bytes 1818628
  45.8 3.3 %slice-start.2 = ((s8[8486912]{0:T(1024)(128)(4,1)}), s8[98304]{0:T(1024)(128)(4,1)S(1)}, s32[]{:S(2)}) async-start(s8[8486912]{0:T(1024)(128)(4,1)} %bitcast.32), calls=%async_computation.7 | async-start | bytes 196608
  49.1 2.8 slice-start.3
  49.1 3.5 %slice-start.4 = ((s8[8486912]{0:T(1024)(128)(4,1)}), s8[4194304]{0:T(1024)(128)(4,1)S(1)}, s32[]{:S(2)}) async-start(s8[8486912]{0:T(1024)(128)(4,1)} %bitcast.34), calls=%async_computation.9 | async-start | bytes 8388608
  50.5 2.1 slice-start.5
  54.0 68.1 %copy-start.12 = (bf16[8,3584]{1,0:T(8,128)(2,1)S(1)}, bf16[8,3584]{1,0:T(8,128)(2,1)}, u32[]{:S(2)}) copy-start(bf16[8,3584]{1,0:T(8,128)(2,1)} %param.9) | copy-start | bytes 172036
  56.1 178.6 %all-gather.4.cloned.1.call-start = ((), (), s32[]{:S(2)}) async-start(), calls=%async_computation.2 | async-start | bytes 2752512 | tf_op jit(solution)/shard_map/all_gather | solution.py:76
  56.7 206.7 %all-gather.6.cloned.1.call-start = ((), (), s32[]{:S(2)}) async-start(), calls=%async_computation.3 | async-start | bytes 2752512 | tf_op jit(solution)/shard_map/all_gather | solution.py:81
  146.4 127.2 %all-gather.8.cloned.1.call-start = ((), (), s32[]{:S(2)}) async-start(), calls=%async_computation.4 | async-start | bytes 2752512 | tf_op jit(solution)/shard_map/all_gather | solution.py:82
  198.1 7.0 %copy-start.2 = (bf16[128,3584]{1,0:T(8,128)(2,1)}, bf16[128,3584]{1,0:T(8,128)(2,1)S(1)}, u32[]{:S(2)}) copy-start(bf16[128,3584]{1,0:T(8,128)(2,1)S(1)} %all_gather.31) | copy-start | bytes 2752516
  198.1 7.0 %copy-start.3 = (bf16[128,3584]{1,0:T(8,128)(2,1)S(1)}, bf16[128,3584]{1,0:T(8,128)(2,1)}, u32[]{:S(2)}) copy-start(bf16[128,3584]{1,0:T(8,128)(2,1)} %all_gather.32) | copy-start | bytes 2752516
  205.1 6.1 %copy-start.6 = (f32[128,1184]{0,1:T(8,128)S(1)}, f32[128,1184]{0,1:T(8,128)}, u32[]{:S(2)}) copy-start(f32[128,1184]{0,1:T(8,128)} %copy-done.5) | copy-start | bytes 1818628
  205.1 6.1 %copy-start.8 = (f32[128,1184]{0,1:T(8,128)S(1)}, f32[128,1184]{0,1:T(8,128)}, u32[]{:S(2)}) copy-start(f32[128,1184]{0,1:T(8,128)} %copy-done.7) | copy-start | bytes 1818628
  205.1 6.1 %copy-start.10 = (f32[128,1184]{0,1:T(8,128)S(1)}, f32[128,1184]{0,1:T(8,128)}, u32[]{:S(2)}) copy-start(f32[128,1184]{0,1:T(8,128)} %copy-done.9) | copy-start | bytes 1818628
  205.1 6.1 %copy-start.11 = (f32[128,1184]{0,1:T(8,128)S(1)}, f32[128,1184]{0,1:T(8,128)}, u32[]{:S(2)}) copy-start(f32[128,1184]{0,1:T(8,128)} %get-tuple-element.7) | copy-start | bytes 1818628
  234.7 20.1 %copy-start.4 = (bf16[256,3584]{1,0:T(8,128)(2,1)S(1)}, bf16[256,3584]{1,0:T(8,128)(2,1)}, u32[]{:S(2)}) copy-start(bf16[256,3584]{1,0:T(8,128)(2,1)} %all-gather.4.cloned.1.call-done) | copy-start | bytes 5505028
Sparse Core Ops, SparseCore 0:
  56.3 65.7 reduce-scatter.1
Sparse Core Ops, SparseCore 1:
  58.7 27.2 all-gather.3
  146.5 36.4 all-gather.5
  205.1 35.3 all-gather.7
where the time goes:
time: 296 us
  blocking collectives  127 us (43%)
  matrix products  81.6 us (28%)
  waiting for transfers between devices  65.9 us (22%)
  between operations  15.9 us (5%)
  other arithmetic  3 us (1%)
    reduce_scatter x1, waiting for transfers between devices, on_device(): lax.psum_scatter(jnp.concatenate([primal, tangent], axis=1), 'fsdp', scat...  65.3 us
    dot_general x4, matrix products, inner_rows(): lax.dot_general(left, right, (((0,), (0,)), ((), ())), preferred_element_...  43.9 us
    all_gather x1, blocking collectives, on_device(): gathered = lax.all_gather(tokens, 'fsdp', axis=0, tiled=True)  26.1 us
    all_gather x1, blocking collectives, on_device(): lax.all_gather(error, 'fsdp', axis=0, tiled=True)  23.4 us
    all_gather x1, blocking collectives, on_device(): lax.all_gather(error_tangent, 'fsdp', axis=0, tiled=True)  20.2 us
    all_gather x1, blocking collectives, on_device(): lax.all_gather(gate_grad_tangent, 'rep', axis=0, tiled=True)  17.2 us
    all_gather x1, blocking collectives, on_device(): lax.all_gather(hidden, 'rep', axis=0, tiled=True)  17 us
    all_gather x1, blocking collectives, on_device(): lax.all_gather(hidden_tangent, 'rep', axis=0, tiled=True)  13.5 us
  transfers between devices with their start and end apart: 4, of which 1 were waited for; matrix products, arithmetic and copies ran while one was open for 17% of the time, Pallas kernels for 0%

commit v1 on v0

--- a/solution.py
+++ b/solution.py
@@ -2,6 +2,11 @@
 import jax.numpy as jnp
 from jax import lax
 from jax.sharding import PartitionSpec as P
+
+
+def gather_over(value, name, dim):
+    sent = jnp.stack([value] * lax.axis_size(name))
+    return jnp.concatenate(lax.all_to_all(sent, name, 0, 0), axis=dim)
 
 
 def silu_parts(gate):
@@ -62,7 +67,7 @@
     error_tangent = summed[:, width:].astype(jnp.bfloat16)
     error_all, error_tangent_all = (
         lax.all_gather(error, "fsdp", axis=0, tiled=True),
-        lax.all_gather(error_tangent, "fsdp", axis=0, tiled=True),
+        gather_over(error_tangent, "fsdp", 0),
     )
     back = jnp.dot(error_all, down_weight.T, preferred_element_type=jnp.float32)
     back_tangent = jnp.dot(

time: 296 us -> 275 us (0.929)
  blocking collectives: 127 us -> 105 us
  matrix products: 81.6 us -> 77.2 us
  starting transfers between devices: 0.17 us -> 4 us
    all_gather x1 -> x0, blocking collectives: 20.2 us -> none  [on_device(): lax.all_gather(error_tangent, 'fsdp', axis=0, tiled=True)]
    all_gather x1, blocking collectives: 17 us -> 9.3 us  [on_device(): lax.all_gather(hidden, 'rep', axis=0, tiled=True)]
    all_gather x1, blocking collectives: 9.9 us -> 17 us  [on_device(): lax.all_gather(up_grad_tangent, 'rep', axis=0, tiled=True)]
    dot_general x1, matrix products: 6.41 us -> 2.64 us  [on_device(): back = jnp.dot(error_all, down_weight.T, preferred_element_type=jnp.float32)]
    all_to_all x0 -> x1, starting transfers between devices: none -> 3.65 us  [gather_over(): return jnp.concatenate(lax.all_to_all(sent, name, 0, 0), axis=dim)]
    all_gather x1, blocking collectives: 13.5 us -> 10.2 us  [on_device(): lax.all_gather(hidden_tangent, 'rep', axis=0, tiled=True)]
  transfers between devices with their start and end apart: 4 -> 5, of which waited for: 1 -> 1; matrix products, arithmetic and copies ran while one was open for 17% -> 17% of each run, Pallas kernels for 0% -> 0%
where the time goes in v1:
time: 275 us; the launch traced here: 274 us
  blocking collectives  105 us (38%)
  matrix products  77.2 us (28%)
  waiting for transfers between devices  66 us (24%)
  between operations  16 us (6%)
  starting transfers between devices  4 us (1%)
  local copies, waits for them, and re-layouts  3.33 us (1%)
  other arithmetic  3 us (1%)
    reduce_scatter x1, waiting for transfers between devices, on_device(): lax.psum_scatter(jnp.concatenate([primal, tangent], axis=1), 'fsdp', scat...  65.4 us
    dot_general x4, matrix products, inner_rows(): lax.dot_general(left, right, (((0,), (0,)), ((), ())), preferred_element_...  43.9 us
    all_gather x1, blocking collectives, on_device(): gathered = lax.all_gather(tokens, 'fsdp', axis=0, tiled=True)  26.1 us
    all_gather x1, blocking collectives, on_device(): lax.all_gather(error, 'fsdp', axis=0, tiled=True)  25.2 us
    all_gather x1, blocking collectives, on_device(): lax.all_gather(gate_grad_tangent, 'rep', axis=0, tiled=True)  17.1 us
    all_gather x1, blocking collectives, on_device(): lax.all_gather(up_grad_tangent, 'rep', axis=0, tiled=True)  17 us
    all_gather x1, blocking collectives, on_device(): lax.all_gather(hidden_tangent, 'rep', axis=0, tiled=True)  10.2 us
    all_gather x1, blocking collectives, on_device(): lax.all_gather(hidden, 'rep', axis=0, tiled=True)  9.3 us
  transfers between devices with their start and end apart: 5, of which 1 were waited for; matrix products, arithmetic and copies ran while one was open for 17% of the time, Pallas kernels for 0%

profile of v1, /device:TPU:0, one launch (start us, length us, event | category | flops | bytes accessed | tf_op | source)
XLA Modules:
  0.0 274.3 jit_solution(199361508943241982)
XLA Ops:
  8.0 26.1 %all_gather.27 = bf16[128,3584]{1,0:T(8,128)(2,1)S(1)} all-gather(bf16[8,3584]{1,0:T(8,128)(2,1)} %param.8), channel_id=1, replica_groups=mesh['rep'=2,'fsdp'=16] {'fsdp'}, dimensions={0}, use_global_device_ids=true | all-gather | bytes 974848 | tf_op jit(solution)/shard_map/all_gather | solution.py:51
  34.2 6.1 %fusion.14 = f32[128,1184]{0,1:T(8,128)S(1)} fusion(bf16[128,3584]{1,0:T(8,128)(2,1)S(1)} %all_gather.27, bf16[3584,1184]{0,1:T(8,128)(2,1)} %param.14), kind=kOutput, calls=%fused_computation.28 | convolution fusion | flops 1086324736 | bytes 10010624 | tf_op jit(solution)/shard_map/dot_general | solution.py:55
  40.4 2.4 fusion.13
  42.8 0.2 slice-done.10
  43.0 2.4 fusion.11
  45.4 0.4 slice-done.13
  45.8 3.2 %multiply_convert_fusion = (bf16[128,1184]{0,1:T(8,128)(2,1)S(1)}, bf16[128,1184]{0,1:T(8,128)(2,1)S(1)}, f32[128,1184]{0,1:T(8,128)}) fusion(f32[128,1184]{0,1:T(8,128)S(1)} %fusion.11, f32[128,1184]{0,1:T(8,128)S(1)} %fusion.14, f32[128,1184]{0,1:T(8,128)S(1)} %fusion.13, bf16[128,3584]{1,0:T(8,128)(2,1)S(1)} %all_gather.27, ...), kind=kOutput, calls=%fused_computation.17 | convolution fusion | flops 1088598016 | bytes 12435456 | tf_op jit(solution)/shard_map/dot_general | solution.py:53
  49.1 1.4 fusion.15
  50.5 1.4 fusion.12
  51.9 0.7 slice-done.7
  52.5 0.1 slice-done.8
  52.6 1.4 convolution_add_fusion.1
  54.0 2.1 pad_maximum_fusion
  56.2 0.5 all-gather.4.cloned.1.call-update
  56.7 65.4 %reduce-scatter.2.cloned.1.call-done = f32[8,7168]{1,0:T(8,128)} async-done(((f32[128,7168]{1,0:T(8,128)}), f32[8,7168]{1,0:T(8,128)}) %reduce-scatter.2.cloned.1.call-update) | async-done | bytes 229392 | tf_op jit(solution)/shard_map/reduce_scatter | solution.py:63
  122.0 0.9 slice.15
  122.9 1.0 stack.2
  123.9 3.6 %all-to-all-start = ((bf16[16,8,3584]{2,1,0:T(8,128)(2,1)}), bf16[16,8,3584]{2,1,0:T(8,128)(2,1)S(1)}, u32[]{:S(2)}, u32[]{:S(2)}) async-start(bf16[16,8,3584]{2,1,0:T(8,128)(2,1)} %stack.2), calls=%async_computation.1 | async-start | bytes 1835008 | tf_op jit(solution)/shard_map/all_to_all | solution.py:9
  127.6 10.2 %all_gather.32 = bf16[256,1184]{0,1:T(8,128)(2,1)S(1)} all-gather(bf16[128,1184]{0,1:T(8,128)(2,1)S(1)} %get-tuple-element.6), channel_id=1, replica_groups=mesh['rep'=2,'fsdp'=16] {'rep'}, dimensions={0}, use_global_device_ids=true | all-gather | bytes 909312 | tf_op jit(solution)/shard_map/all_gather | solution.py:85
  137.8 9.3 %all_gather.34 = bf16[256,1184]{0,1:T(8,128)(2,1)S(1)} all-gather(bf16[128,1184]{0,1:T(8,128)(2,1)S(1)} %get-tuple-element.5), channel_id=1, replica_groups=mesh['rep'=2,'fsdp'=16] {'rep'}, dimensions={0}, use_global_device_ids=true | all-gather | bytes 909312 | tf_op jit(solution)/shard_map/all_gather | solution.py:84
  147.1 0.9 fusion.8
  148.0 25.2 %all_gather.28 = bf16[128,3584]{1,0:T(8,128)(2,1)} all-gather(bf16[8,3584]{1,0:T(8,128)(2,1)S(1)} %fusion.8), channel_id=1, replica_groups=mesh['rep'=2,'fsdp'=16] {'fsdp'}, dimensions={0}, use_global_device_ids=true | all-gather | bytes 974848 | tf_op jit(solution)/shard_map/all_gather | solution.py:69
  173.2 0.2 all-gather.8.cloned.1.call-start
  173.5 6.4 %fusion.9 = f32[128,1184]{0,1:T(8,128)S(1)} fusion(bf16[1184,3584]{1,0:T(8,128)(2,1)} %param.12, bf16[16,8,3584]{2,1,0:T(8,128)(2,1)S(1)} %all-to-all-done), kind=kOutput, calls=%fused_computation.23 | convolution fusion | flops 1086324736 | bytes 10010624 | tf_op jit(solution)/shard_map/dot_general | solution.py:73
  180.0 5.9 %convolution_add_fusion.2 = f32[128,1184]{0,1:T(8,128)S(1)} fusion(f32[128,1184]{0,1:T(8,128)S(1)} %fusion.9, bf16[128,3584]{1,0:T(8,128)(2,1)S(1)} %copy-done.3, bf16[1184,3584]{1,0:T(8,128)(2,1)} %param.15), kind=kOutput, calls=%fused_computation.5 | convolution fusion | flops 1086476288 | bytes 10616832 | tf_op jit(solution)/shard_map/dot_general | solution.py:75
  186.0 2.6 add_convert_fusion
  188.6 17.1 %all_gather.29 = bf16[256,1184]{0,1:T(8,128)(2,1)S(1)} all-gather(bf16[128,1184]{0,1:T(8,128)(2,1)S(1)} %get-tuple-element.4), channel_id=1, replica_groups=mesh['rep'=2,'fsdp'=16] {'rep'}, dimensions={0}, use_global_device_ids=true | all-gather | bytes 909312 | tf_op jit(solution)/shard_map/all_gather | solution.py:82
  205.8 10.3 %convolution_bitcast_fusion.1 = f32[3584,1184]{0,1:T(8,128)} fusion(bf16[256,1184]{0,1:T(8,128)(2,1)S(1)} %all_gather.29, bf16[256,3584]{1,0:T(8,128)(2,1)} %all-gather.4.cloned.1.call-done), kind=kOutput, calls=%fused_computation.2 | convolution fusion | flops 2172649472 | bytes 19415040 | tf_op jit(solution)/shard_map/dot_general | solution.py:20
  216.0 17.0 %all_gather.31 = bf16[256,1184]{0,1:T(8,128)(2,1)S(1)} all-gather(bf16[128,1184]{0,1:T(8,128)(2,1)S(1)} %get-tuple-element.3), channel_id=1, replica_groups=mesh['rep'=2,'fsdp'=16] {'rep'}, dimensions={0}, use_global_device_ids=true | all-gather | bytes 909312 | tf_op jit(solution)/shard_map/all_gather | solution.py:83
  233.0 8.6 %convolution_bitcast_fusion = f32[3584,1184]{0,1:T(8,128)} fusion(bf16[256,1184]{0,1:T(8,128)(2,1)S(1)} %all_gather.31, bf16[256,3584]{1,0:T(8,128)(2,1)S(1)} %copy-done.4), kind=kOutput, calls=%fused_computation.1 | convolution fusion | flops 2172649472 | bytes 19415040 | tf_op jit(solution)/shard_map/dot_general | solution.py:20
  241.6 10.1 %fusion.16 = f32[1184,3584]{1,0:T(8,128)} fusion(bf16[256,1184]{0,1:T(8,128)(2,1)S(1)} %all_gather.32, bf16[256,3584]{1,0:T(8,128)(2,1)} %all-gather.6.cloned.1.call-done), kind=kOutput, calls=%fused_computation.30 | convolution fusion | flops 2172649472 | bytes 19415040 | tf_op jit(solution)/shard_map/dot_general | solution.py:20
  251.7 15.0 %convolution_add_fusion = f32[1184,3584]{1,0:T(8,128)} fusion(f32[1184,3584]{1,0:T(8,128)} %fusion.16, bf16[256,1184]{0,1:T(8,128)(2,1)S(1)} %all_gather.34, bf16[256,3584]{1,0:T(8,128)(2,1)} %all-gather.8.cloned.1.call-done), kind=kOutput, calls=%fused_computation | convolution fusion | flops 2176892928 | bytes 36388864 | tf_op jit(solution)/shard_map/dot_general | solution.py:20
  (67 shorter events, 0.4 us)
Async XLA Ops:
  8.0 114.0 %reduce-scatter.2.cloned.1.call-start = ((), (), s32[]{:S(2)}) async-start(), calls=%async_computation.2 | async-start | bytes 3899392 | tf_op jit(solution)/shard_map/reduce_scatter | solution.py:63
  34.2 11.2 %copy-start = (bf16[128,3584]{1,0:T(8,128)(2,1)}, bf16[128,3584]{1,0:T(8,128)(2,1)S(1)}, u32[]{:S(2)}) copy-start(bf16[128,3584]{1,0:T(8,128)(2,1)S(1)} %all_gather.27) | copy-start | bytes 2752516
  34.2 6.2 %copy-start.1 = (bf16[3584,1184]{0,1:T(8,128)(2,1)S(1)}, bf16[3584,1184]{0,1:T(8,128)(2,1)}, u32[]{:S(2)}) copy-start(bf16[3584,1184]{0,1:T(8,128)(2,1)} %param.13) | copy-start | bytes 25460740
  34.2 8.6 %slice-start.9 = ((s8[8486912]{0:T(1024)(128)(4,1)}), s8[4194304]{0:T(1024)(128)(4,1)S(1)}, s32[]{:S(2)}) async-start(s8[8486912]{0:T(1024)(128)(4,1)} %bitcast.40), calls=%async_computation.15 | async-start | bytes 8388608
  34.2 8.8 %slice-start.10 = ((s8[8486912]{0:T(1024)(128)(4,1)}), s8[4194304]{0:T(1024)(128)(4,1)S(1)}, s32[]{:S(2)}) async-start(s8[8486912]{0:T(1024)(128)(4,1)} %bitcast.40), calls=%async_computation.16 | async-start | bytes 8388608
  40.4 5.0 %copy-start.5 = (f32[128,1184]{0,1:T(8,128)}, f32[128,1184]{0,1:T(8,128)S(1)}, u32[]{:S(2)}) copy-start(f32[128,1184]{0,1:T(8,128)S(1)} %fusion.14) | copy-start | bytes 1818628
  40.4 2.6 slice-start.11
  40.4 5.0 %slice-start.12 = ((s8[8486912]{0:T(1024)(128)(4,1)}), s8[4194304]{0:T(1024)(128)(4,1)S(1)}, s32[]{:S(2)}) async-start(s8[8486912]{0:T(1024)(128)(4,1)} %bitcast.42), calls=%async_computation.18 | async-start | bytes 8388608
  40.4 5.4 %slice-start.13 = ((s8[8486912]{0:T(1024)(128)(4,1)}), s8[4194304]{0:T(1024)(128)(4,1)S(1)}, s32[]{:S(2)}) async-start(s8[8486912]{0:T(1024)(128)(4,1)} %bitcast.42), calls=%async_computation.19 | async-start | bytes 8388608
  43.0 2.4 copy-start.7
  43.0 2.8 %slice-start.14 = ((s8[8486912]{0:T(1024)(128)(4,1)}), s8[98304]{0:T(1024)(128)(4,1)S(1)}, s32[]{:S(2)}) async-start(s8[8486912]{0:T(1024)(128)(4,1)} %bitcast.42), calls=%async_computation.20 | async-start | bytes 196608
  43.0 6.0 %slice-start = ((s8[8486912]{0:T(1024)(128)(4,1)}), s8[4194304]{0:T(1024)(128)(4,1)S(1)}, s32[]{:S(2)}) async-start(s8[8486912]{0:T(1024)(128)(4,1)} %bitcast.34), calls=%async_computation.6 | async-start | bytes 8388608
  43.0 6.0 %slice-start.1 = ((s8[8486912]{0:T(1024)(128)(4,1)}), s8[4194304]{0:T(1024)(128)(4,1)S(1)}, s32[]{:S(2)}) async-start(s8[8486912]{0:T(1024)(128)(4,1)} %bitcast.34), calls=%async_computation.7 | async-start | bytes 8388608
  45.8 3.2 %copy-start.9 = (f32[128,1184]{0,1:T(8,128)}, f32[128,1184]{0,1:T(8,128)S(1)}, u32[]{:S(2)}) copy-start(f32[128,1184]{0,1:T(8,128)S(1)} %fusion.11) | copy-start | bytes 1818628
  45.8 3.2 %slice-start.2 = ((s8[8486912]{0:T(1024)(128)(4,1)}), s8[98304]{0:T(1024)(128)(4,1)S(1)}, s32[]{:S(2)}) async-start(s8[8486912]{0:T(1024)(128)(4,1)} %bitcast.34), calls=%async_computation.8 | async-start | bytes 196608
  49.0 2.8 %slice-start.6 = ((s8[8486912]{0:T(1024)(128)(4,1)}), s8[4194304]{0:T(1024)(128)(4,1)S(1)}, s32[]{:S(2)}) async-start(s8[8486912]{0:T(1024)(128)(4,1)} %bitcast.38), calls=%async_computation.12 | async-start | bytes 8388608
  49.1 3.5 %slice-start.7 = ((s8[8486912]{0:T(1024)(128)(4,1)}), s8[4194304]{0:T(1024)(128)(4,1)S(1)}, s32[]{:S(2)}) async-start(s8[8486912]{0:T(1024)(128)(4,1)} %bitcast.38), calls=%async_computation.13 | async-start | bytes 8388608
  54.0 93.1 %copy-start.12 = (bf16[8,3584]{1,0:T(8,128)(2,1)S(1)}, bf16[8,3584]{1,0:T(8,128)(2,1)}, u32[]{:S(2)}) copy-start(bf16[8,3584]{1,0:T(8,128)(2,1)} %param.9) | copy-start | bytes 172036
  56.1 149.7 %all-gather.4.cloned.1.call-start = ((), (), s32[]{:S(2)}) async-start(), calls=%async_computation.3 | async-start | bytes 2752512 | tf_op jit(solution)/shard_map/all_gather | solution.py:81
  123.9 49.5 %all-to-all-start = ((bf16[16,8,3584]{2,1,0:T(8,128)(2,1)}), bf16[16,8,3584]{2,1,0:T(8,128)(2,1)S(1)}, u32[]{:S(2)}, u32[]{:S(2)}) async-start(bf16[16,8,3584]{2,1,0:T(8,128)(2,1)} %stack.2), calls=%async_computation.1 | async-start | bytes 1835008 | tf_op jit(solution)/shard_map/all_to_all | solution.py:9
  127.6 114.0 %all-gather.6.cloned.1.call-start = ((), (), s32[]{:S(2)}) async-start(), calls=%async_computation.4 | async-start | bytes 2752512 | tf_op jit(solution)/shard_map/all_gather | solution.py:86
  173.2 6.7 %copy-start.3 = (bf16[128,3584]{1,0:T(8,128)(2,1)S(1)}, bf16[128,3584]{1,0:T(8,128)(2,1)}, u32[]{:S(2)}) copy-start(bf16[128,3584]{1,0:T(8,128)(2,1)} %all_gather.28) | copy-start | bytes 2752516
  173.2 78.5 %all-gather.8.cloned.1.call-start = ((), (), s32[]{:S(2)}) async-start(), calls=%async_computation.5 | async-start | bytes 2752512 | tf_op jit(solution)/shard_map/all_gather | solution.py:87
  173.4 6.5 %copy-start.2 = (bf16[16,8,3584]{2,1,0:T(8,128)(2,1)}, bf16[16,8,3584]{2,1,0:T(8,128)(2,1)S(1)}, u32[]{:S(2)}) copy-start(bf16[16,8,3584]{2,1,0:T(8,128)(2,1)S(1)} %all-to-all-done) | copy-start | bytes 2752516
  173.5 12.5 %slice-start.3 = ((s8[8486912]{0:T(1024)(128)(4,1)}), s8[4194304]{0:T(1024)(128)(4,1)S(1)}, s32[]{:S(2)}) async-start(s8[8486912]{0:T(1024)(128)(4,1)} %bitcast.36), calls=%async_computation.9 | async-start | bytes 8388608
  173.5 12.5 %slice-start.4 = ((s8[8486912]{0:T(1024)(128)(4,1)}), s8[4194304]{0:T(1024)(128)(4,1)S(1)}, s32[]{:S(2)}) async-start(s8[8486912]{0:T(1024)(128)(4,1)} %bitcast.36), calls=%async_computation.10 | async-start | bytes 8388608
  179.9 6.0 %slice-start.5 = ((s8[8486912]{0:T(1024)(128)(4,1)}), s8[98304]{0:T(1024)(128)(4,1)S(1)}, s32[]{:S(2)}) async-start(s8[8486912]{0:T(1024)(128)(4,1)} %bitcast.36), calls=%async_computation.11 | async-start | bytes 196608
  179.9 6.0 %copy-start.6 = (f32[128,1184]{0,1:T(8,128)S(1)}, f32[128,1184]{0,1:T(8,128)}, u32[]{:S(2)}) copy-start(f32[128,1184]{0,1:T(8,128)} %copy-done.5) | copy-start | bytes 1818628
  179.9 6.0 %copy-start.8 = (f32[128,1184]{0,1:T(8,128)S(1)}, f32[128,1184]{0,1:T(8,128)}, u32[]{:S(2)}) copy-start(f32[128,1184]{0,1:T(8,128)} %copy-done.7) | copy-start | bytes 1818628
  180.0 6.0 %copy-start.10 = (f32[128,1184]{0,1:T(8,128)S(1)}, f32[128,1184]{0,1:T(8,128)}, u32[]{:S(2)}) copy-start(f32[128,1184]{0,1:T(8,128)} %copy-done.9) | copy-start | bytes 1818628
  180.0 6.0 %copy-start.11 = (f32[128,1184]{0,1:T(8,128)S(1)}, f32[128,1184]{0,1:T(8,128)}, u32[]{:S(2)}) copy-start(f32[128,1184]{0,1:T(8,128)} %get-tuple-element.7) | copy-start | bytes 1818628
  205.8 27.2 %copy-start.4 = (bf16[256,3584]{1,0:T(8,128)(2,1)S(1)}, bf16[256,3584]{1,0:T(8,128)(2,1)}, u32[]{:S(2)}) copy-start(bf16[256,3584]{1,0:T(8,128)(2,1)} %all-gather.4.cloned.1.call-done) | copy-start | bytes 5505028
  (1 other events, 2.1 us)
Sparse Core Ops, SparseCore 0:
  56.2 65.7 reduce-scatter.1
Sparse Core Ops, SparseCore 1:
  58.7 27.2 all-gather.3
  173.3 33.7 all-gather.5
  208.5 36.5 all-gather.7
